TPU v7x, 32 devices: a whole 2x2x4 slice. The times are simulated.
32 devices in a mesh: dp: 8 (over z, y), tensor: 4 (over x, core).
Axes of the slice: x: 2, y: 2, z: 4, core: 2. Of those that a mesh axis runs over, the one named last changes fastest.
Arguments:
- tokens_in: bfloat16 [1024, 4096], P(('dp', 'tensor')), may hold values from -6 to 6
- grad_out: bfloat16 [1024, 4096], P(('dp', 'tensor')), may hold values from -6 to 6
- gate_pre: bfloat16 [1024, 7168], P('dp', 'tensor'), may hold values from -6 to 6
- up_pre: bfloat16 [1024, 7168], P('dp', 'tensor'), may hold values from -6 to 6
- gate_weight: bfloat16 [4096, 7168], P('dp', 'tensor'), may hold values from -0.09375 to 0.09375
- up_weight: bfloat16 [4096, 7168], P('dp', 'tensor'), may hold values from -0.09375 to 0.09375
- down_weight: bfloat16 [7168, 4096], P('tensor', 'dp'), may hold values from -0.0625 to 0.0625
- norm_gain: float32 [4096], replicated, may hold values from 0.1 to 1.9
Outputs:
- input_grad: bfloat16 [1024, 4096], P(('dp', 'tensor'))
- gain_grad: float32 [4096], replicated
- down_grad: bfloat16 [7168, 4096], P('tensor', 'dp')
All inputs are finite; a program needn't handle non-finite values.
Results may differ from a plain program's by a relative error of at most 0.015.
Values may be sent and summed in bfloat16 or wider, within the bound.
A program may use at most 64 MiB of HBM per device.

v0:
```python
import jax
import jax.numpy as jnp
from jax import lax
from jax.sharding import PartitionSpec as P


def per_device(
    tokens_in, grad_out, gate_pre, up_pre, gate_weight, up_weight, down_weight, norm_gain
):
    group_out = lax.all_gather(grad_out, "tensor", axis=0, tiled=True)
    gate_value = gate_pre.astype(jnp.float32)
    up_value = up_pre.astype(jnp.float32)
    gate_sigmoid = jax.nn.sigmoid(gate_value)
    gate_silu = gate_value * gate_sigmoid
    act = (gate_silu * up_value).astype(jnp.bfloat16)
    grad_act = lax.dot_general(
        group_out,
        lax.all_gather(down_weight, "dp", axis=1, tiled=True),
        (((1,), (1,)), ((), ())),
        preferred_element_type=jnp.float32,
    )
    grad_gate = (
        grad_act * up_value * gate_sigmoid * (1.0 + gate_value * (1.0 - gate_sigmoid))
    ).astype(jnp.bfloat16)
    grad_up = (grad_act * gate_silu).astype(jnp.bfloat16)
    stacked = jnp.stack((grad_gate, grad_up))
    local_weight = jnp.stack((gate_weight, up_weight))
    every_group = jnp.einsum(
        "grf,gdf->rd",
        lax.all_gather(stacked, "dp", axis=1, tiled=True),
        local_weight,
        preferred_element_type=jnp.float32,
    ).astype(jnp.bfloat16)
    partial_value = lax.all_to_all(
        every_group, "dp", split_axis=0, concat_axis=1, tiled=True
    ).astype(jnp.float32)
    grad_norm = lax.psum_scatter(
        partial_value.astype(jnp.bfloat16), "tensor", scatter_dimension=0, tiled=True
    ).astype(jnp.float32)
    every_out = lax.all_to_all(group_out, "dp", split_axis=1, concat_axis=0, tiled=True)
    total = lax.dot_general(
        lax.all_gather(act, "dp", axis=0, tiled=True),
        every_out,
        (((0,), (0,)), ((), ())),
        preferred_element_type=jnp.float32,
    )
    down_grad = total.astype(jnp.bfloat16)
    inputs = tokens_in.astype(jnp.float32)
    inv_rms = lax.rsqrt(jnp.mean(inputs * inputs, axis=1, keepdims=True) + 1e-05)
    normed = inputs * inv_rms
    gain_grad = lax.psum(jnp.sum(grad_norm * normed, axis=0), ("dp", "tensor"))
    scaled = grad_norm * norm_gain
    inner = jnp.mean(scaled * normed, axis=1, keepdims=True)
    input_grad = (grad_out.astype(jnp.float32) + inv_rms * (scaled - normed * inner)).astype(
        jnp.bfloat16
    )
    return (input_grad, gain_grad, down_grad)


def solution(mesh):
    return jax.shard_map(
        per_device,
        mesh=mesh,
        in_specs=(
            P(("dp", "tensor"), None),
            P(("dp", "tensor"), None),
            P("dp", "tensor"),
            P("dp", "tensor"),
            P("dp", "tensor"),
            P("dp", "tensor"),
            P("tensor", "dp"),
            P(),
        ),
        out_specs=(P(("dp", "tensor"), None), P(), P("tensor", "dp")),
        check_vma=False,
    )
```

profile of v0, /device:TPU:0, one launch (start us, length us, event | category | flops | bytes accessed | tf_op | source)
XLA Modules:
  0.0 534.6 jit_solution(6595157011614198800)
XLA Ops:
  7.2 0.0 all-gather.5.cloned.1.call-start
  7.2 0.7 all-gather.5.cloned.1.call-update
  7.9 0.0 all-gather.7.cloned.1.call-start
  7.9 0.7 all-gather.7.cloned.1.call-update
  8.6 0.0 copy-start.4
  8.7 0.0 all-gather.9.cloned.1.call-start
  8.7 20.3 %all-gather.5.cloned.1.call-done = bf16[128,4096]{1,0:T(8,128)(2,1)} async-done(((bf16[32,4096]{1,0:T(8,128)(2,1)}), bf16[128,4096]{1,0:T(8,128)(2,1)}) %all-gather.5.cloned.1.call-update) | async-done | bytes 1048592 | tf_op jit(solution)/shard_map/all_gather | solution.py:10
  29.0 203.8 %all-gather.7.cloned.1.call-done = bf16[1792,4096]{1,0:T(8,128)(2,1)} async-done(((bf16[1792,512]{1,0:T(8,128)(2,1)}), bf16[1792,4096]{1,0:T(8,128)(2,1)}) %all-gather.7.cloned.1.call-update) | async-done | bytes 14680080 | tf_op jit(solution)/shard_map/all_gather | solution.py:18
  232.8 11.5 %fusion.24 = (bf16[1,128,1792]{2,1,0:T(8,128)(2,1)S(1)}, bf16[1,128,1792]{2,1,0:T(8,128)(2,1)S(1)}, bf16[128,1792]{1,0:T(8,128)(2,1)}) fusion(bf16[128,1792]{1,0:T(8,128)(2,1)} %param.10, bf16[128,1792]{1,0:T(8,128)(2,1)} %param.11, bf16[128,4096]{1,0:T(8,128)(2,1)} %all-gather.5.cloned.1.call-done, bf16[1792,4096]{1,0:T(8,128)(2,1)} %all-gather.7.cloned.1.call-done), kind=kOutput, calls=%fused_computation.35 | convolution fusion | flops 1882947584 | bytes 18022400 | tf_op jit(solution)/shard_map/dot_general | solution.py:16
  244.3 1.0 pad_maximum_fusion
  245.3 0.0 all-gather.9.cloned.1.call-update
  245.3 0.0 all-gather.11.cloned.1.call-start
  245.4 0.5 all-gather.11.cloned.1.call-update
  245.9 109.2 %all-gather.9.cloned.1.call-done = bf16[2,1024,1792]{2,1,0:T(8,128)(2,1)} async-done(((bf16[2,128,1792]{2,1,0:T(8,128)(2,1)}), bf16[2,1024,1792]{2,1,0:T(8,128)(2,1)}) %all-gather.9.cloned.1.call-update) | async-done | bytes 7340048 | tf_op jit(solution)/shard_map/all_gather | solution.py:30
  355.1 0.0 copy-done.4
  355.1 0.0 copy-start.2
  355.1 8.6 %bitcast_convert_fusion = bf16[1024,512]{1,0:T(8,128)(2,1)} fusion(bf16[2,1024,1792]{2,1,0:T(8,128)(2,1)} %all-gather.9.cloned.1.call-done, bf16[1,512,1792]{2,1,0:T(8,128)(2,1)S(1)} %bitcast.24, bf16[1,512,1792]{2,1,0:T(8,128)(2,1)} %bitcast.25), kind=kOutput, calls=%fused_computation.5 | convolution fusion | flops 3760455680 | bytes 12058624 | tf_op jit(solution)/shard_map/grf,gdf->rd/dot_general | solution.py:28
  363.8 3.6 all-to-all-start
  367.3 0.0 copy-done.2
  367.3 0.0 copy-start
  367.3 1.3 copy.17
  368.7 36.0 %all-to-all-done = bf16[8,128,512]{2,1,0:T(8,128)(2,1)S(1)} async-done(((bf16[8,128,512]{2,1,0:T(8,128)(2,1)}), bf16[8,128,512]{2,1,0:T(8,128)(2,1)S(1)}, u32[]{:S(2)}, u32[]{:S(2)}) %all-to-all-start) | async-done | bytes 1048608 | tf_op jit(solution)/shard_map/all_to_all | solution.py:34
  404.6 3.6 all-to-all-start.1
  408.2 0.0 reduce-scatter.2.cloned.1.call-start
  408.2 1.1 copy.19
  409.3 0.0 reduce-scatter.2.cloned.1.call-update
  409.3 0.0 copy-done
  409.3 0.2 fusion.21
  409.5 48.8 %all-to-all-done.1 = bf16[128,8,512]{0,2,1:T(8,128)(2,1)S(1)} async-done(((bf16[128,8,512]{0,2,1:T(8,128)(2,1)}), bf16[128,8,512]{0,2,1:T(8,128)(2,1)S(1)}, u32[]{:S(2)}, u32[]{:S(2)}) %all-to-all-start.1) | async-done | bytes 1048608 | tf_op jit(solution)/shard_map/all_to_all | solution.py:40
  458.3 0.5 copy.18
  458.9 0.5 all-gather.11.cloned.1.call-done
  459.4 0.0 copy-start.3
  459.4 0.0 copy-start.1
  459.4 5.4 %convolution_convert_fusion = bf16[1792,512]{1,0:T(8,128)(2,1)} fusion(bf16[1024,1792]{1,0:T(8,128)(2,1)} %all-gather.11.cloned.1.call-done, bf16[1024,512]{1,0:T(8,128)(2,1)S(1)} %bitcast.23), kind=kOutput, calls=%fused_computation.4 | convolution fusion | flops 1879965696 | bytes 6553600 | tf_op jit(solution)/shard_map/dot_general | solution.py:41
  464.8 20.7 %reduce-scatter.2.cloned.1.call-done = bf16[32,4096]{1,0:T(8,128)(2,1)} async-done(((bf16[128,4096]{1,0:T(8,128)(2,1)}), bf16[32,4096]{1,0:T(8,128)(2,1)}) %reduce-scatter.2.cloned.1.call-update) | async-done | bytes 262160 | tf_op jit(solution)/shard_map/reduce_scatter | solution.py:37
  485.5 0.0 copy-done.3
  485.5 1.3 fusion.22
  486.8 39.4 %psum.7 = f32[4096]{0:T(1024)} all-reduce(f32[4096]{0:T(1024)S(1)} %get-tuple-element.3), channel_id=1, replica_groups=mesh['dp'=8,'tensor'=4] {'dp','tensor'}, use_global_device_ids=true, to_apply=%region_4.0 | all-reduce | flops 4096 | bytes 32768 | tf_op jit(solution)/shard_map/psum | solution.py:51
  526.2 0.0 copy-done.1
  526.2 1.9 fusion.19
  (2 shorter events, 0.0 us)
Async XLA Ops:
  7.2 21.8 %all-gather.5.cloned.1.call-start = ((), (), s32[]{:S(2)}) async-start(), calls=%async_computation.3 | async-start | bytes 1310720 | tf_op jit(solution)/shard_map/all_gather | solution.py:10
  7.9 224.9 %all-gather.7.cloned.1.call-start = ((), (), s32[]{:S(2)}) async-start(), calls=%async_computation.4 | async-start | bytes 16515072 | tf_op jit(solution)/shard_map/all_gather | solution.py:18
  8.6 346.5 %copy-start.4 = (bf16[512,1792]{1,0:T(8,128)(2,1)S(1)}, bf16[512,1792]{1,0:T(8,128)(2,1)}, u32[]{:S(2)}) copy-start(bf16[512,1792]{1,0:T(8,128)(2,1)} %param.13) | copy-start | bytes 5505028
  8.7 346.5 %all-gather.9.cloned.1.call-start = ((), (), s32[]{:S(2)}) async-start(), calls=%async_computation.5 | async-start | bytes 8257536 | tf_op jit(solution)/shard_map/all_gather | solution.py:30
  245.3 214.1 %all-gather.11.cloned.1.call-start = ((), (), s32[]{:S(2)}) async-start(), calls=%async_computation.7 | async-start | bytes 4128768 | tf_op jit(solution)/shard_map/all_gather | solution.py:42
  355.1 12.2 %copy-start.2 = (bf16[128,4096]{1,0:T(8,128)(2,1)S(1)}, bf16[128,4096]{1,0:T(8,128)(2,1)}, u32[]{:S(2)}) copy-start(bf16[128,4096]{1,0:T(8,128)(2,1)} %all-gather.5.cloned.1.call-done) | copy-start | bytes 3145732
  363.8 40.9 %all-to-all-start = ((bf16[8,128,512]{2,1,0:T(8,128)(2,1)}), bf16[8,128,512]{2,1,0:T(8,128)(2,1)S(1)}, u32[]{:S(2)}, u32[]{:S(2)}) async-start(bf16[8,128,512]{2,1,0:T(8,128)(2,1)} %bitcast.5), calls=%async_computation | async-start | bytes 2097152 | tf_op jit(solution)/shard_map/all_to_all | solution.py:34
  367.3 42.0 %copy-start = (bf16[32,4096]{1,0:T(8,128)(2,1)S(1)}, bf16[32,4096]{1,0:T(8,128)(2,1)}, u32[]{:S(2)}) copy-start(bf16[32,4096]{1,0:T(8,128)(2,1)} %param.8) | copy-start | bytes 786436
  404.6 53.7 %all-to-all-start.1 = ((bf16[128,8,512]{0,2,1:T(8,128)(2,1)}), bf16[128,8,512]{0,2,1:T(8,128)(2,1)S(1)}, u32[]{:S(2)}, u32[]{:S(2)}) async-start(bf16[128,8,512]{0,2,1:T(8,128)(2,1)} %bitcast.7), calls=%async_computation.2 | async-start | bytes 2097152 | tf_op jit(solution)/shard_map/all_to_all | solution.py:40
  408.2 77.3 %reduce-scatter.2.cloned.1.call-start = ((), (), s32[]{:S(2)}) async-start(), calls=%async_computation.6 | async-start | bytes 1310720 | tf_op jit(solution)/shard_map/reduce_scatter | solution.py:37
  459.4 26.2 %copy-start.3 = (f32[4096]{0:T(1024)S(1)}, f32[4096]{0:T(1024)}, u32[]{:S(2)}) copy-start(f32[4096]{0:T(1024)} %param.15) | copy-start | bytes 49156
  459.4 66.8 %copy-start.1 = (bf16[32,4096]{1,0:T(8,128)(2,1)S(1)}, bf16[32,4096]{1,0:T(8,128)(2,1)}, u32[]{:S(2)}) copy-start(bf16[32,4096]{1,0:T(8,128)(2,1)} %param.9) | copy-start | bytes 786436
Sparse Core Ops, SparseCore 0:
  9.5 19.4 all-gather.4
  31.0 201.6 all-gather.6
  245.4 109.6 all-gather.8
  357.2 102.1 all-gather.10
  461.7 23.7 reduce-scatter.1
where the time goes:
time: 535 us
  waiting for transfers between devices  441 us (82%)
  blocking collectives  39.4 us (7%)
  matrix products  25.6 us (5%)
  between operations  13.8 us (3%)
  starting transfers between devices  7.31 us (1%)
    all_gather x1, waiting for transfers between devices, per_device(): lax.all_gather(down_weight, 'dp', axis=1, tiled=True)  204 us
    all_gather x1, waiting for transfers between devices, per_device(): lax.all_gather(stacked, 'dp', axis=1, tiled=True)  109 us
    all_to_all x1, waiting for transfers between devices, per_device(): lax.all_to_all(group_out, 'dp', split_axis=1, concat_axis=0, tiled=True)  48.8 us
    psum x1, blocking collectives, per_device(): gain_grad = lax.psum(jnp.sum(grad_norm * normed, axis=0), ('dp', 'tensor'))  39.4 us
    all_to_all x1, waiting for transfers between devices, per_device(): lax.all_to_all(every_group, 'dp', split_axis=0, concat_axis=1, tiled=True)  36 us
    reduce_scatter x1, waiting for transfers between devices, per_device(): lax.psum_scatter(partial_value.astype(jnp.bfloat16), 'tensor', scatter_di...  20.7 us
    all_gather x1, waiting for transfers between devices, per_device(): group_out = lax.all_gather(grad_out, 'tensor', axis=0, tiled=True)  20.3 us
    dot_general x1, matrix products, per_device(): lax.dot_general(group_out, lax.all_gather(down_weight, 'dp', axis=1, tile...  11.5 us
  transfers between devices with their start and end apart: 7, of which 7 were waited for; matrix products, arithmetic and copies ran while one was open for 3% of the time, Pallas kernels for 0%

commit v1 on v0

v1 whole, which is shorter than its diff:
```python
import functools

import jax
import jax.numpy as jnp
from jax import lax
from jax.experimental import pallas as pl
from jax.experimental.pallas import tpu as pltpu
from jax.sharding import PartitionSpec as P

MESH = pl.DeviceIdType.MESH
F32 = jnp.float32
BF16 = jnp.bfloat16
NT = (((1,), (1,)), ((), ()))
TN = (((0,), (0,)), ((), ()))


def split_line(n_dp):
    assert n_dp % 4 == 0
    return n_dp // 2


def body(
    n_dp,
    n_t,
    chunks,
    tok_ref,
    out_ref,
    gate_ref,
    up_ref,
    wg_ref,
    wu_ref,
    wd_ref,
    gain_ref,
    ig_ref,
    gg_out_ref,
    dg_ref,
    x4,
    x2,
    aall,
    ysend,
    yrecv,
    own,
    zsend,
    zin,
    gg,
    npb,
    nrv,
    gs,
    fin,
    gbuf,
    hbuf,
    s1_s,
    s1_r,
    s2_s,
    s2_r,
    ys_s,
    ys_r,
    a_s,
    a_r,
    z_s,
    z_r,
    b_s,
    b_r,
    n_s,
    n_r,
    f_s,
    f_r,
    g_s,
    g_r,
    h_s,
    h_r,
):
    r, width = tok_ref.shape
    rows, hidden = gate_ref.shape
    cols = wg_ref.shape[0]
    line = split_line(n_dp)
    rc = rows // chunks
    d = lax.axis_index("dp")
    t = lax.axis_index("tensor")
    z = d // 2
    y = d % 2
    other = 1 - y
    pair = z * 2 + other

    def loop(n, f, start=0):
        def step(i, carry):
            f(i)
            return carry

        lax.fori_loop(start, n, step, 0)

    def dp_peer(k):
        return lax.rem(d + k, n_dp)

    def t_peer(k):
        return lax.rem(t + k, n_t)

    def rcopy(src, dst, ss, rs, dd, tt):
        return pltpu.make_async_remote_copy(
            src_ref=src,
            dst_ref=dst,
            send_sem=ss,
            recv_sem=rs,
            device_id={"dp": dd, "tensor": tt},
            device_id_type=MESH,
        )

    barrier = pltpu.get_barrier_semaphore()
    loop(
        n_dp,
        lambda k: pl.semaphore_signal(
            barrier, inc=1, device_id={"dp": dp_peer(k), "tensor": t}, device_id_type=MESH
        ),
        1,
    )
    loop(
        n_t,
        lambda k: pl.semaphore_signal(
            barrier, inc=1, device_id={"dp": d, "tensor": t_peer(k)}, device_id_type=MESH
        ),
        1,
    )
    pl.semaphore_wait(barrier, n_dp + n_t - 2)

    def col(i):
        return pl.ds(pl.multiple_of(i * cols, cols), cols)

    def first(k, tgt):
        return rcopy(
            out_ref.at[:, col(tgt)], x4.at[d, t], s1_s.at[k], s1_r.at[d], tgt, t
        )

    def first_in(src):
        return rcopy(out_ref.at[:, col(0)], x4.at[src, t], s1_s.at[0], s1_r.at[src], d, t)

    loop(n_dp, lambda k: first(k, dp_peer(k)).start(), 1)

    def second(src, j):
        return rcopy(
            x4.at[src, t], x4.at[src, t], s2_s.at[src, j], s2_r.at[src, t], d, t_peer(j)
        )

    def second_in(src, tt):
        return rcopy(x4.at[src, tt], x4.at[src, tt], s2_s.at[src, 0], s2_r.at[src, tt], d, t)

    def second_own(j):
        return rcopy(
            out_ref.at[:, col(d)], x4.at[d, t], s2_s.at[d, j], s2_r.at[d, t], d, t_peer(j)
        )

    x4[d, t] = out_ref[:, col(d)]
    loop(n_t, lambda j: second_own(j).start(), 1)

    gate = gate_ref[...].astype(F32)
    aall[d] = (gate * jax.nn.sigmoid(gate) * up_ref[...].astype(F32)).astype(BF16)

    def up_copy(unit, ss, rs, src, c):
        return rcopy(unit(src * 2 + y, c), unit(src * 2 + y, c), ss.at[0, src, c], rs.at[0, src, c], d + 2, t)

    def down_copy(unit, ss, rs, src, c):
        return rcopy(unit(src * 2 + y, c), unit(src * 2 + y, c), ss.at[1, src, c], rs.at[1, src, c], d - 2, t)

    def pair_copy(unit, ss, rs, src, c):
        return rcopy(unit(src * 2 + y, c), unit(src * 2 + y, c), ss.at[2, src, c], rs.at[2, src, c], pair, t)

    def arrived(unit, ss, rs, way, src, side, c):
        u = unit(src * 2 + side, c)
        rcopy(u, u, ss.at[way, src, c], rs.at[way, src, c], d, t).wait_recv()

    def gather_own(unit, ss, rs, c):
        @pl.when(z < line - 1)
        def _():
            up_copy(unit, ss, rs, z, c).start()

        @pl.when(z > 0)
        def _():
            down_copy(unit, ss, rs, z, c).start()

        pair_copy(unit, ss, rs, z, c).start()

    def gather_step(unit, ss, rs, s, n_c):
        for c in range(n_c):
            low, high = z - s, z + s

            @pl.when(low >= 0)
            def _():
                arrived(unit, ss, rs, 0, low, y, c)

                @pl.when(z < line - 1)
                def _():
                    up_copy(unit, ss, rs, low, c).start()

                pair_copy(unit, ss, rs, low, c).start()

            @pl.when(high < line)
            def _():
                arrived(unit, ss, rs, 1, high, y, c)

                @pl.when(z > 0)
                def _():
                    down_copy(unit, ss, rs, high, c).start()

                pair_copy(unit, ss, rs, high, c).start()

    def gather_drain(unit, ss, rs, n_c):
        def one(src):
            for c in range(n_c):

                @pl.when((src <= z) & (z < line - 1))
                def _():
                    up_copy(unit, ss, rs, src, c).wait_send()

                @pl.when((src >= z) & (z > 0))
                def _():
                    down_copy(unit, ss, rs, src, c).wait_send()

                pair_copy(unit, ss, rs, src, c).wait_send()

        loop(line, one)

    def act_unit(i, c):
        return aall.at[i]

    gather_own(act_unit, a_s, a_r, 0)

    def relay(k):
        src = lax.rem(d + n_dp - k, n_dp)
        first_in(src).wait_recv()
        loop(n_t, lambda j: second(src, j).start(), 1)

    loop(n_dp, relay, 1)

    def settle(src):
        loop(n_t, lambda j: second_in(src, t_peer(j)).wait_recv(), 1)
        x2[src] = x4[src].astype(F32).reshape(rows, cols).astype(BF16)

    loop(n_dp, settle)

    def cs(c):
        return pl.ds(c * rc, rc)

    def pair_part(zz, c):
        return rcopy(
            ysend.at[zz, cs(c)], yrecv.at[zz, cs(c)], ys_s.at[zz, c], ys_r.at[zz, c], pair, t
        )

    def partial(i):
        return lax.dot_general(x2[i], wd_ref[...], NT, preferred_element_type=F32)

    def send_parts(p):
        def make(q):
            zz = jnp.where(q == 0, line - 1 - p, p)
            ysend[zz] = partial(zz * 2 + other).astype(BF16)

        loop(2, make)
        for c in range(chunks):
            pair_part(line - 1 - p, c).start()
            pair_part(p, c).start()

    loop(line // 2, send_parts)

    def keep(zz):
        own[zz] = partial(zz * 2 + y)

    loop(line, keep)

    loop(line, lambda s: gather_step(act_unit, a_s, a_r, s, 1), 1)

    def line_part(way, zz, c):
        return rcopy(
            zsend.at[zz, cs(c)],
            zin.at[way, zz, cs(c)],
            z_s.at[zz, c],
            z_r.at[way, zz, c],
            d + 2 - 4 * way,
            t,
        )

    def line_in(way, zz, c):
        rcopy(
            zsend.at[zz, cs(c)], zin.at[way, zz, cs(c)], z_s.at[zz, c], z_r.at[way, zz, c], d, t
        ).wait_recv()

    def reduce_one(zz, c):
        pair_part(zz, c).wait_recv()
        own[zz, cs(c)] += yrecv[zz, cs(c)].astype(F32)

        def send_on(way, has_before):
            @pl.when(has_before)
            def _():
                line_in(way, zz, c)
                own[zz, cs(c)] += zin[way, zz, cs(c)].astype(F32)

            zsend[zz, cs(c)] = own[zz, cs(c)].astype(BF16)
            line_part(way, zz, c).start()

        @pl.when(zz > z)
        def _():
            send_on(0, z > 0)

        @pl.when(zz < z)
        def _():
            send_on(1, z < line - 1)

    def reduce_pairs(p):
        for c in range(chunks):
            reduce_one(line - 1 - p, c)
            reduce_one(p, c)

    loop(line // 2, reduce_pairs)

    def grad_unit(i, c):
        return gg.at[i, :, cs(c)]

    for c in range(chunks):

        @pl.when(z > 0)
        def _():
            line_in(0, z, c)
            own[z, cs(c)] += zin[0, z, cs(c)].astype(F32)

        @pl.when(z < line - 1)
        def _():
            line_in(1, z, c)
            own[z, cs(c)] += zin[1, z, cs(c)].astype(F32)

        grad_act = own[z, cs(c)]
        gate = gate_ref[cs(c), :].astype(F32)
        sig = jax.nn.sigmoid(gate)
        gg[d, 0, cs(c)] = (
            grad_act * up_ref[cs(c), :].astype(F32) * sig * (1.0 + gate * (1.0 - sig))
        ).astype(BF16)
        gg[d, 1, cs(c)] = (grad_act * (gate * sig)).astype(BF16)
        gather_own(grad_unit, b_s, b_r, c)

    loop(line, lambda src: arrived(act_unit, a_s, a_r, 2, src, other, 0))
    tile = 256 if hidden % 256 == 0 else hidden

    def down_tile(i):
        if tile == hidden:
            sl = slice(None)
        else:
            sl = pl.ds(pl.multiple_of(i * tile, tile), tile)
        left = aall[:, :, sl].reshape(n_dp * rows, tile)
        right = x2[...].reshape(n_dp * rows, cols)
        res = lax.dot_general(left, right, TN, preferred_element_type=F32).astype(BF16)
        if tile == hidden:
            dg_ref[...] = res
        else:
            dg_ref[sl, :] = res

    loop(hidden // tile, down_tile)

    def norm_copy(i, j):
        tt = t_peer(j)
        return rcopy(npb.at[i, tt], nrv.at[i, t], n_s.at[i, j], n_r.at[i, t], d, tt)

    def norm_block(i):
        part = lax.dot_general(gg[i, 0], wg_ref[...], NT, preferred_element_type=F32)
        part = part + lax.dot_general(gg[i, 1], wu_ref[...], NT, preferred_element_type=F32)
        npb[i] = part.reshape(n_t, r, cols).astype(BF16)
        loop(n_t, lambda j: norm_copy(i, j).start(), 1)

    def visit(s):
        @pl.when((s > 0) & (s < line))
        def _():
            gather_step(grad_unit, b_s, b_r, s, chunks)

        def one(q):
            dist = s - q // 2
            src = jnp.where(q % 2 == 0, z - dist, z + dist)
            ok = (dist >= 0) & (src >= 0) & (src < line) & ((dist > 0) | (q % 2 == 0))

            @pl.when(ok)
            def _():
                @pl.when(q >= 2)
                def _():
                    for c in range(chunks):
                        arrived(grad_unit, b_s, b_r, 2, src, other, c)

                norm_block(src * 2 + jnp.where(q >= 2, other, y))

        loop(4, one)

    loop(line + 1, visit)

    def fin_copy(i):
        return rcopy(gs.at[i], fin.at[d], f_s.at[i], f_r.at[d], i, t)

    def combine(k):
        i = dp_peer(k)

        def add(j, acc):
            tt = t_peer(j)
            rcopy(npb.at[i, tt], nrv.at[i, tt], n_s.at[i, 0], n_r.at[i, tt], d, t).wait_recv()
            return acc + nrv[i, tt].astype(F32)

        acc = lax.fori_loop(1, n_t, add, npb[i, t].astype(F32)).astype(BF16)

        @pl.when(k > 0)
        def _():
            gs[i] = acc
            fin_copy(i).start()

        @pl.when(k == 0)
        def _():
            fin[d] = acc

    loop(n_dp, combine)

    total = jnp.zeros((r, 1), F32)
    for i in range(n_dp):
        v = tok_ref[:, i * cols : (i + 1) * cols].astype(F32)
        total = total + jnp.sum(v * v, axis=1, keepdims=True)
    inv = lax.rsqrt(total / width + 1e-05)

    def fin_in(k):
        i = dp_peer(k)
        rcopy(gs.at[i], fin.at[i], f_s.at[i], f_r.at[i], d, t).wait_recv()

    loop(n_dp, fin_in, 1)

    inner = jnp.zeros((r, 1), F32)
    for i in range(n_dp):
        sl = slice(i * cols, (i + 1) * cols)
        prod = fin[i].astype(F32) * (tok_ref[:, sl].astype(F32) * inv)
        gbuf[t, :, sl] = jnp.sum(prod, axis=0, keepdims=True)
        inner = inner + jnp.sum(prod * gain_ref[:, sl], axis=1, keepdims=True)
    inner = inner / width

    def gain_copy(j):
        return rcopy(gbuf.at[t], gbuf.at[t], g_s.at[j], g_r.at[t], d, t_peer(j))

    loop(n_t, lambda j: gain_copy(j).start(), 1)
    for i in range(n_dp):
        sl = slice(i * cols, (i + 1) * cols)
        scaled = fin[i].astype(F32) * gain_ref[:, sl]
        normed = tok_ref[:, sl].astype(F32) * inv
        ig_ref[:, sl] = (
            out_ref[:, sl].astype(F32) + inv * (scaled - normed * inner)
        ).astype(BF16)

    def gain_in(j):
        tt = t_peer(j)
        rcopy(gbuf.at[tt], gbuf.at[tt], g_s.at[0], g_r.at[tt], d, t).wait_recv()

    loop(n_t, gain_in, 1)
    hbuf[d] = jnp.sum(gbuf[...], axis=0)

    def all_copy(k):
        return rcopy(hbuf.at[d], hbuf.at[d], h_s.at[k], h_r.at[d], dp_peer(k), t)

    loop(n_dp, lambda k: all_copy(k).start(), 1)

    def all_in(k):
        i = dp_peer(k)
        rcopy(hbuf.at[i], hbuf.at[i], h_s.at[0], h_r.at[i], d, t).wait_recv()

    loop(n_dp, all_in, 1)
    gg_out_ref[...] = jnp.sum(hbuf[...], axis=0)

    loop(n_dp, lambda k: first(k, dp_peer(k)).wait_send(), 1)
    loop(n_dp, lambda i: loop(n_t, lambda j: second(i, j).wait_send(), 1))
    gather_drain(act_unit, a_s, a_r, 1)
    gather_drain(grad_unit, b_s, b_r, chunks)

    def drain_parts(zz):
        for c in range(chunks):
            pair_part(zz, c).wait_send()

            @pl.when(zz != z)
            def _():
                line_part(0, zz, c).wait_send()

    loop(line, drain_parts)
    loop(n_dp, lambda i: loop(n_t, lambda j: norm_copy(i, j).wait_send(), 1))
    loop(n_dp, lambda k: fin_copy(dp_peer(k)).wait_send(), 1)
    loop(n_t, lambda j: gain_copy(j).wait_send(), 1)
    loop(n_dp, lambda k: all_copy(k).wait_send(), 1)


def per_device(
    n_dp, n_t, tokens_in, grad_out, gate_pre, up_pre, gate_weight, up_weight, down_weight, norm_gain
):
    r, width = tokens_in.shape
    rows, hidden = gate_pre.shape
    cols = gate_weight.shape[0]
    line = split_line(n_dp)
    chunks = 4 if rows % 64 == 0 else 1
    dma = pltpu.SemaphoreType.DMA
    vmem = pl.BlockSpec(memory_space=pltpu.VMEM)
    input_grad, gain_grad, down_grad = pl.pallas_call(
        functools.partial(body, n_dp, n_t, chunks),
        out_shape=(
            jax.ShapeDtypeStruct((r, width), BF16),
            jax.ShapeDtypeStruct((1, width), F32),
            jax.ShapeDtypeStruct((hidden, cols), BF16),
        ),
        in_specs=[vmem] * 8,
        out_specs=(vmem, vmem, vmem),
        scratch_shapes=[
            pltpu.VMEM((n_dp, n_t, r, cols), BF16),
            pltpu.VMEM((n_dp, rows, cols), BF16),
            pltpu.VMEM((n_dp, rows, hidden), BF16),
            pltpu.VMEM((line, rows, hidden), BF16),
            pltpu.VMEM((line, rows, hidden), BF16),
            pltpu.VMEM((line, rows, hidden), F32),
            pltpu.VMEM((line, rows, hidden), BF16),
            pltpu.VMEM((2, line, rows, hidden), BF16),
            pltpu.VMEM((n_dp, 2, rows, hidden), BF16),
            pltpu.VMEM((n_dp, n_t, r, cols), BF16),
            pltpu.VMEM((n_dp, n_t, r, cols), BF16),
            pltpu.VMEM((n_dp, r, cols), BF16),
            pltpu.VMEM((n_dp, r, cols), BF16),
            pltpu.VMEM((n_t, 1, width), F32),
            pltpu.VMEM((n_dp, 1, width), F32),
            dma((n_dp,)),
            dma((n_dp,)),
            dma((n_dp, n_t)),
            dma((n_dp, n_t)),
            dma((line, chunks)),
            dma((line, chunks)),
            dma((3, line, 1)),
            dma((3, line, 1)),
            dma((line, chunks)),
            dma((2, line, chunks)),
            dma((3, line, chunks)),
            dma((3, line, chunks)),
            dma((n_dp, n_t)),
            dma((n_dp, n_t)),
            dma((n_dp,)),
            dma((n_dp,)),
            dma((n_t,)),
            dma((n_t,)),
            dma((n_dp,)),
            dma((n_dp,)),
        ],
        compiler_params=pltpu.CompilerParams(
            collective_id=0, has_side_effects=True, vmem_limit_bytes=63 * 2**20
        ),
    )(
        tokens_in,
        grad_out,
        gate_pre,
        up_pre,
        gate_weight,
        up_weight,
        down_weight,
        norm_gain.reshape(1, width),
    )
    return (input_grad, gain_grad.reshape(width), down_grad)


def solution(mesh):
    return jax.shard_map(
        functools.partial(per_device, mesh.shape["dp"], mesh.shape["tensor"]),
        mesh=mesh,
        in_specs=(
            P(("dp", "tensor"), None),
            P(("dp", "tensor"), None),
            P("dp", "tensor"),
            P("dp", "tensor"),
            P("dp", "tensor"),
            P("dp", "tensor"),
            P("tensor", "dp"),
            P(),
        ),
        out_specs=(P(("dp", "tensor"), None), P(), P("tensor", "dp")),
        check_vma=False,
    )
```

time: 535 us -> 205 us (0.38)
  waiting for transfers between devices: 441 us -> 0 us
  Pallas kernels: 0 us -> 199 us
  blocking collectives: 39.4 us -> 0 us
  matrix products: 25.6 us -> 0 us
  between operations: 13.8 us -> 0.64 us
  starting transfers between devices: 7.31 us -> 0 us
    all_gather x4 -> x0, waiting for transfers between devices: 334 us -> none  [the longest x1 204 us: per_device(): lax.all_gather(down_weight, 'dp', axis=1, tiled=True)]
    pallas_call x0 -> x1, Pallas kernels: none -> 199 us  [per_device(): pl.pallas_call(functools.partial(body, n_dp, n_t, chunks), out_shape=(jax...]
    all_to_all x2 -> x0, waiting for transfers between devices: 84.8 us -> none  [the longest x1 48.8 us: per_device(): lax.all_to_all(group_out, 'dp', split_axis=1, concat_axis=0, tiled=True)]
    psum x1 -> x0, blocking collectives: 39.4 us -> none  [per_device(): gain_grad = lax.psum(jnp.sum(grad_norm * normed, axis=0), ('dp', 'tensor'))]
    dot_general x3 -> x0, matrix products: 25.6 us -> none  [the longest x1 11.5 us: per_device(): lax.dot_general(group_out, lax.all_gather(down_weight, 'dp', axis=1, tile...]
    reduce_scatter x1 -> x0, waiting for transfers between devices: 20.7 us -> none  [per_device(): lax.psum_scatter(partial_value.astype(jnp.bfloat16), 'tensor', scatter_di...]
    all_to_all x2 -> x0, starting transfers between devices: 7.12 us -> none  [the longest x1 3.56 us: per_device(): lax.all_to_all(every_group, 'dp', split_axis=0, concat_axis=1, tiled=True)]
    unnamed x10 -> x3, local copies, waits for them, and re-layouts: 0.02 us -> 5.84 us
  transfers between devices with their start and end apart: 7 -> 0, of which waited for: 7 -> 0; matrix products, arithmetic and copies ran while one was open for 3% -> 0% of each run, Pallas kernels for 0% -> 0%
where the time goes in v1:
time: 205 us
  Pallas kernels  199 us (97%)
  local copies, waits for them, and re-layouts  5.84 us (3%)
    pallas_call x1, Pallas kernels, per_device(): pl.pallas_call(functools.partial(body, n_dp, n_t, chunks), out_shape=(jax...  199 us
    unnamed x3, local copies, waits for them, and re-layouts  5.84 us

profile of v1, /device:TPU:0, one launch (start us, length us, event | category | flops | bytes accessed | tf_op | source)
XLA Modules:
  0.0 205.0 jit_solution(17194119905331279179)
XLA Ops:
  0.6 198.5 %shard_map.103 = (bf16[32,4096]{1,0:T(8,128)(2,1)}, f32[1,4096]{1,0:T(1,128)}, bf16[1792,512]{1,0:T(8,128)(2,1)}) custom-call(bf16[32,4096]{1,0:T(8,128)(2,1)} %tok_ref.1, bf16[32,4096]{1,0:T(8,128)(2,1)} %out_ref.1, bf16[128,1792]{1,0:T(8,128)(2,1)} %gate_ref.1, bf16[128,1792]{1,0:T(8,128)(2,1)} %up_ref.1, bf16[512,1792]{1,0:T(8,128)(2,1)} %wg_ref.1, ...), custom_call_target="tpu_custom_call" | custom-call | tf_op jit(solution)/shard_map/pallas_call | solution.py:492
  199.1 1.7 copy.14
  200.8 1.3 copy.15
  202.1 2.8 %copy.16 = bf16[1792,512]{1,0:T(8,128)(2,1)} copy(bf16[1792,512]{1,0:T(8,128)(2,1)} %get-tuple-element.14) | data formatting | bytes 3670016

commit v2 on v1

--- a/solution.py
+++ b/solution.py
@@ -8,6 +8,7 @@
 from jax.sharding import PartitionSpec as P
 
 MESH = pl.DeviceIdType.MESH
+W_CHUNKS = 4
 F32 = jnp.float32
 BF16 = jnp.bfloat16
 NT = (((1,), (1,)), ((), ()))
@@ -43,6 +44,7 @@
     zsend,
     zin,
     gg,
+    wrecv,
     npb,
     nrv,
     gs,
@@ -61,6 +63,8 @@
     z_r,
     b_s,
     b_r,
+    w_s,
+    w_r,
     n_s,
     n_r,
     f_s,
@@ -154,74 +158,88 @@
     gate = gate_ref[...].astype(F32)
     aall[d] = (gate * jax.nn.sigmoid(gate) * up_ref[...].astype(F32)).astype(BF16)
 
-    def up_copy(unit, ss, rs, src, c):
-        return rcopy(unit(src * 2 + y, c), unit(src * 2 + y, c), ss.at[0, src, c], rs.at[0, src, c], d + 2, t)
-
-    def down_copy(unit, ss, rs, src, c):
-        return rcopy(unit(src * 2 + y, c), unit(src * 2 + y, c), ss.at[1, src, c], rs.at[1, src, c], d - 2, t)
-
-    def pair_copy(unit, ss, rs, src, c):
-        return rcopy(unit(src * 2 + y, c), unit(src * 2 + y, c), ss.at[2, src, c], rs.at[2, src, c], pair, t)
+    w_rows = cols // W_CHUNKS
+
+    def weight_copy(n):
+        a, c = n % 2, n // 2
+        src = (wg_ref, wu_ref)[a].at[pl.ds(c * w_rows, w_rows)]
+        return rcopy(
+            src, wrecv.at[a, pl.ds(c * w_rows, w_rows)], w_s.at[a, c], w_r.at[a, c], pair, t
+        )
+
+    def up_copy(unit, ss, rs, way, src, side, c):
+        u = unit(src, side, c)
+        return rcopy(u, u, ss.at[way, src, c], rs.at[way, src, c], d + 2, t)
+
+    def down_copy(unit, ss, rs, way, src, side, c):
+        u = unit(src, side, c)
+        return rcopy(u, u, ss.at[way + 1, src, c], rs.at[way + 1, src, c], d - 2, t)
 
     def arrived(unit, ss, rs, way, src, side, c):
-        u = unit(src * 2 + side, c)
+        u = unit(src, side, c)
         rcopy(u, u, ss.at[way, src, c], rs.at[way, src, c], d, t).wait_recv()
 
-    def gather_own(unit, ss, rs, c):
+    def gather_own(unit, ss, rs, way, side, c):
         @pl.when(z < line - 1)
         def _():
-            up_copy(unit, ss, rs, z, c).start()
+            up_copy(unit, ss, rs, way, z, side, c).start()
 
         @pl.when(z > 0)
         def _():
-            down_copy(unit, ss, rs, z, c).start()
-
-        pair_copy(unit, ss, rs, z, c).start()
-
-    def gather_step(unit, ss, rs, s, n_c):
-        for c in range(n_c):
-            low, high = z - s, z + s
-
-            @pl.when(low >= 0)
+            down_copy(unit, ss, rs, way, z, side, c).start()
+
+    def gather_step(unit, ss, rs, way, side, s, c, then=None):
+        low, high = z - s, z + s
+
+        @pl.when(low >= 0)
+        def _():
+            arrived(unit, ss, rs, way, low, side, c)
+
+            @pl.when(z < line - 1)
             def _():
-                arrived(unit, ss, rs, 0, low, y, c)
-
-                @pl.when(z < line - 1)
-                def _():
-                    up_copy(unit, ss, rs, low, c).start()
-
-                pair_copy(unit, ss, rs, low, c).start()
-
-            @pl.when(high < line)
+                up_copy(unit, ss, rs, way, low, side, c).start()
+
+            if then is not None:
+                then(low)
+
+        @pl.when(high < line)
+        def _():
+            arrived(unit, ss, rs, way + 1, high, side, c)
+
+            @pl.when(z > 0)
             def _():
-                arrived(unit, ss, rs, 1, high, y, c)
-
-                @pl.when(z > 0)
-                def _():
-                    down_copy(unit, ss, rs, high, c).start()
-
-                pair_copy(unit, ss, rs, high, c).start()
-
-    def gather_drain(unit, ss, rs, n_c):
+                down_copy(unit, ss, rs, way, high, side, c).start()
+
+            if then is not None:
+                then(high)
+
+    def gather_drain(unit, ss, rs, way, side, c):
         def one(src):
-            for c in range(n_c):
-
-                @pl.when((src <= z) & (z < line - 1))
-                def _():
-                    up_copy(unit, ss, rs, src, c).wait_send()
-
-                @pl.when((src >= z) & (z > 0))
-                def _():
-                    down_copy(unit, ss, rs, src, c).wait_send()
-
-                pair_copy(unit, ss, rs, src, c).wait_send()
+            @pl.when((src <= z) & (z < line - 1))
+            def _():
+                up_copy(unit, ss, rs, way, src, side, c).wait_send()
+
+            @pl.when((src >= z) & (z > 0))
+            def _():
+                down_copy(unit, ss, rs, way, src, side, c).wait_send()
 
         loop(line, one)
 
-    def act_unit(i, c):
-        return aall.at[i]
-
-    gather_own(act_unit, a_s, a_r, 0)
+    half = rows // 2
+
+    def act_unit(src, side, c):
+        return aall.at[src * 2 + side, pl.ds(c * half, half)]
+
+    def act_pair(src, c):
+        u = act_unit(src, y, c)
+        return rcopy(u, u, a_s.at[2, src, c], a_r.at[2, src, c], pair, t)
+
+    act_pair(z, 1).start()
+    gather_own(act_unit, a_s, a_r, 0, y, 0)
+    gather_own(act_unit, a_s, a_r, 0, y, 1)
+    act_pair(z, 0).start()
+    for n in range(2):
+        weight_copy(n).start()
 
     def relay(k):
         src = lax.rem(d + n_dp - k, n_dp)
@@ -229,6 +247,8 @@
         loop(n_t, lambda j: second(src, j).start(), 1)
 
     loop(n_dp, relay, 1)
+    arrived(act_unit, a_s, a_r, 2, z, other, 1)
+    gather_own(act_unit, a_s, a_r, 3, other, 1)
 
     def settle(src):
         loop(n_t, lambda j: second_in(src, t_peer(j)).wait_recv(), 1)
@@ -264,7 +284,18 @@
 
     loop(line, keep)
 
-    loop(line, lambda s: gather_step(act_unit, a_s, a_r, s, 1), 1)
+    weight_copy(2).start()
+
+    def act_step(s):
+        gather_step(
+            act_unit, a_s, a_r, 0, y, s, 0, lambda src: act_pair(src, 0).start()
+        )
+        gather_step(act_unit, a_s, a_r, 0, y, s, 1)
+        gather_step(act_unit, a_s, a_r, 3, other, s, 1)
+
+    loop(line, act_step, 1)
+    for n in range(3, 2 * W_CHUNKS):
+        weight_copy(n).start()
 
     def line_part(way, zz, c):
         return rcopy(
@@ -309,8 +340,8 @@
 
     loop(line // 2, reduce_pairs)
 
-    def grad_unit(i, c):
-        return gg.at[i, :, cs(c)]
+    def grad_unit(src, side, c):
+        return gg.at[src, :, cs(c)]
 
     for c in range(chunks):
 
@@ -327,11 +358,11 @@
         grad_act = own[z, cs(c)]
         gate = gate_ref[cs(c), :].astype(F32)
         sig = jax.nn.sigmoid(gate)
-        gg[d, 0, cs(c)] = (
+        gg[z, 0, cs(c)] = (
             grad_act * up_ref[cs(c), :].astype(F32) * sig * (1.0 + gate * (1.0 - sig))
         ).astype(BF16)
-        gg[d, 1, cs(c)] = (grad_act * (gate * sig)).astype(BF16)
-        gather_own(grad_unit, b_s, b_r, c)
+        gg[z, 1, cs(c)] = (grad_act * (gate * sig)).astype(BF16)
+        gather_own(grad_unit, b_s, b_r, 0, y, c)
 
     loop(line, lambda src: arrived(act_unit, a_s, a_r, 2, src, other, 0))
     tile = 256 if hidden % 256 == 0 else hidden
@@ -351,62 +382,81 @@
 
     loop(hidden // tile, down_tile)
 
-    def norm_copy(i, j):
+    def norm_copy(side, i, j):
         tt = t_peer(j)
-        return rcopy(npb.at[i, tt], nrv.at[i, t], n_s.at[i, j], n_r.at[i, t], d, tt)
-
-    def norm_block(i):
+        return rcopy(
+            npb.at[side, i, tt], nrv.at[side, i, t], n_s.at[side, i, j], n_r.at[side, i, t], d, tt
+        )
+
+    def norm_own(i):
         part = lax.dot_general(gg[i, 0], wg_ref[...], NT, preferred_element_type=F32)
         part = part + lax.dot_general(gg[i, 1], wu_ref[...], NT, preferred_element_type=F32)
-        npb[i] = part.reshape(n_t, r, cols).astype(BF16)
-        loop(n_t, lambda j: norm_copy(i, j).start(), 1)
-
-    def visit(s):
-        @pl.when((s > 0) & (s < line))
-        def _():
-            gather_step(grad_unit, b_s, b_r, s, chunks)
-
-        def one(q):
-            dist = s - q // 2
-            src = jnp.where(q % 2 == 0, z - dist, z + dist)
-            ok = (dist >= 0) & (src >= 0) & (src < line) & ((dist > 0) | (q % 2 == 0))
-
-            @pl.when(ok)
-            def _():
-                @pl.when(q >= 2)
-                def _():
-                    for c in range(chunks):
-                        arrived(grad_unit, b_s, b_r, 2, src, other, c)
-
-                norm_block(src * 2 + jnp.where(q >= 2, other, y))
-
-        loop(4, one)
-
-    loop(line + 1, visit)
-
-    def fin_copy(i):
-        return rcopy(gs.at[i], fin.at[d], f_s.at[i], f_r.at[d], i, t)
-
-    def combine(k):
-        i = dp_peer(k)
-
+        npb[y, i] = part.reshape(n_t, r, cols).astype(BF16)
+        loop(n_t, lambda j: norm_copy(y, i, j).start(), 1)
+
+    def norm_other(p):
+        two = pl.ds(2 * p, 2)
+        part = lax.dot_general(
+            gg[two, 0].reshape(2 * rows, hidden), wrecv[0], NT, preferred_element_type=F32
+        )
+        part = part + lax.dot_general(
+            gg[two, 1].reshape(2 * rows, hidden), wrecv[1], NT, preferred_element_type=F32
+        )
+        npb[other, two] = part.reshape(2, n_t, r, cols).astype(BF16)
+        loop(2, lambda q: loop(n_t, lambda j: norm_copy(other, 2 * p + q, j).start(), 1))
+
+    def fin_copy(side, i):
+        return rcopy(
+            gs.at[side, i], fin.at[z, side], f_s.at[side, i], f_r.at[side, z], i * 2 + y, t
+        )
+
+    def combine(side, i):
         def add(j, acc):
             tt = t_peer(j)
-            rcopy(npb.at[i, tt], nrv.at[i, tt], n_s.at[i, 0], n_r.at[i, tt], d, t).wait_recv()
-            return acc + nrv[i, tt].astype(F32)
-
-        acc = lax.fori_loop(1, n_t, add, npb[i, t].astype(F32)).astype(BF16)
-
-        @pl.when(k > 0)
-        def _():
-            gs[i] = acc
-            fin_copy(i).start()
-
-        @pl.when(k == 0)
-        def _():
-            fin[d] = acc
-
-    loop(n_dp, combine)
+            rcopy(
+                npb.at[side, i, tt], nrv.at[side, i, tt], n_s.at[side, i, 0], n_r.at[side, i, tt], d, t
+            ).wait_recv()
+            return acc + nrv[side, i, tt].astype(F32)
+
+        acc = lax.fori_loop(1, n_t, add, npb[side, i, t].astype(F32)).astype(BF16)
+
+        @pl.when(i != z)
+        def _():
+            gs[side, i] = acc
+            fin_copy(side, i).start()
+
+        @pl.when(i == z)
+        def _():
+            fin[z, side] = acc
+
+    def at_distance(dist, f):
+        def one(q):
+            src = jnp.where(q == 0, z - dist, z + dist)
+
+            @pl.when((src >= 0) & (src < line) & ((dist > 0) | (q == 0)))
+            def _():
+                f(src)
+
+        loop(2, one)
+
+    def visit(s):
+        @pl.when(s > 0)
+        def _():
+            for c in range(chunks):
+                gather_step(grad_unit, b_s, b_r, 0, y, s, c)
+
+        at_distance(s, norm_own)
+
+        @pl.when(s > 0)
+        def _():
+            at_distance(s - 1, lambda src: combine(y, src))
+
+    loop(line, visit)
+    for n in range(2 * W_CHUNKS):
+        weight_copy(n).wait_recv()
+    loop(line // 2, norm_other)
+    at_distance(line - 1, lambda src: combine(y, src))
+    loop(line, lambda i: combine(other, i))
 
     total = jnp.zeros((r, 1), F32)
     for i in range(n_dp):
@@ -415,15 +465,21 @@
     inv = lax.rsqrt(total / width + 1e-05)
 
     def fin_in(k):
-        i = dp_peer(k)
-        rcopy(gs.at[i], fin.at[i], f_s.at[i], f_r.at[i], d, t).wait_recv()
-
-    loop(n_dp, fin_in, 1)
+        i = lax.rem(z + k, line)
+
+        def one(side):
+            rcopy(
+                gs.at[side, i], fin.at[i, side], f_s.at[side, i], f_r.at[side, i], d, t
+            ).wait_recv()
+
+        loop(2, one)
+
+    loop(line, fin_in, 1)
 
     inner = jnp.zeros((r, 1), F32)
     for i in range(n_dp):
         sl = slice(i * cols, (i + 1) * cols)
-        prod = fin[i].astype(F32) * (tok_ref[:, sl].astype(F32) * inv)
+        prod = fin[i // 2, i % 2].astype(F32) * (tok_ref[:, sl].astype(F32) * inv)
         gbuf[t, :, sl] = jnp.sum(prod, axis=0, keepdims=True)
         inner = inner + jnp.sum(prod * gain_ref[:, sl], axis=1, keepdims=True)
     inner = inner / width
@@ -434,7 +490,7 @@
     loop(n_t, lambda j: gain_copy(j).start(), 1)
     for i in range(n_dp):
         sl = slice(i * cols, (i + 1) * cols)
-        scaled = fin[i].astype(F32) * gain_ref[:, sl]
+        scaled = fin[i // 2, i % 2].astype(F32) * gain_ref[:, sl]
         normed = tok_ref[:, sl].astype(F32) * inv
         ig_ref[:, sl] = (
             out_ref[:, sl].astype(F32) + inv * (scaled - normed * inner)
@@ -461,8 +517,15 @@
 
     loop(n_dp, lambda k: first(k, dp_peer(k)).wait_send(), 1)
     loop(n_dp, lambda i: loop(n_t, lambda j: second(i, j).wait_send(), 1))
-    gather_drain(act_unit, a_s, a_r, 1)
-    gather_drain(grad_unit, b_s, b_r, chunks)
+    for c in range(2):
+        gather_drain(act_unit, a_s, a_r, 0, y, c)
+    gather_drain(act_unit, a_s, a_r, 3, other, 1)
+    loop(line, lambda src: act_pair(src, 0).wait_send())
+    act_pair(z, 1).wait_send()
+    for n in range(2 * W_CHUNKS):
+        weight_copy(n).wait_send()
+    for c in range(chunks):
+        gather_drain(grad_unit, b_s, b_r, 0, y, c)
 
     def drain_parts(zz):
         for c in range(chunks):
@@ -473,8 +536,12 @@
                 line_part(0, zz, c).wait_send()
 
     loop(line, drain_parts)
-    loop(n_dp, lambda i: loop(n_t, lambda j: norm_copy(i, j).wait_send(), 1))
-    loop(n_dp, lambda k: fin_copy(dp_peer(k)).wait_send(), 1)
+
+    def drain_norm(side):
+        loop(line, lambda i: loop(n_t, lambda j: norm_copy(side, i, j).wait_send(), 1))
+        loop(line, lambda k: fin_copy(side, lax.rem(z + k, line)).wait_send(), 1)
+
+    loop(2, drain_norm)
     loop(n_t, lambda j: gain_copy(j).wait_send(), 1)
     loop(n_dp, lambda k: all_copy(k).wait_send(), 1)
 
@@ -507,11 +574,12 @@
             pltpu.VMEM((line, rows, hidden), F32),
             pltpu.VMEM((line, rows, hidden), BF16),
             pltpu.VMEM((2, line, rows, hidden), BF16),
-            pltpu.VMEM((n_dp, 2, rows, hidden), BF16),
-            pltpu.VMEM((n_dp, n_t, r, cols), BF16),
-            pltpu.VMEM((n_dp, n_t, r, cols), BF16),
-            pltpu.VMEM((n_dp, r, cols), BF16),
-            pltpu.VMEM((n_dp, r, cols), BF16),
+            pltpu.VMEM((line, 2, rows, hidden), BF16),
+            pltpu.VMEM((2, cols, hidden), BF16),
+            pltpu.VMEM((2, line, n_t, r, cols), BF16),
+            pltpu.VMEM((2, line, n_t, r, cols), BF16),
+            pltpu.VMEM((2, line, r, cols), BF16),
+            pltpu.VMEM((line, 2, r, cols), BF16),
             pltpu.VMEM((n_t, 1, width), F32),
             pltpu.VMEM((n_dp, 1, width), F32),
             dma((n_dp,)),
@@ -520,16 +588,18 @@
             dma((n_dp, n_t)),
             dma((line, chunks)),
             dma((line, chunks)),
-            dma((3, line, 1)),
-            dma((3, line, 1)),
+            dma((5, line, 2)),
+            dma((5, line, 2)),
             dma((line, chunks)),
             dma((2, line, chunks)),
-            dma((3, line, chunks)),
-            dma((3, line, chunks)),
-            dma((n_dp, n_t)),
-            dma((n_dp, n_t)),
-            dma((n_dp,)),
-            dma((n_dp,)),
+            dma((2, line, chunks)),
+            dma((2, line, chunks)),
+            dma((2, W_CHUNKS)),
+            dma((2, W_CHUNKS)),
+            dma((2, line, n_t)),
+            dma((2, line, n_t)),
+            dma((2, line)),
+            dma((2, line)),
             dma((n_t,)),
             dma((n_t,)),
             dma((n_dp,)),

time: 205 us -> 188 us (0.917)
  Pallas kernels: 199 us -> 182 us
    pallas_call x1, Pallas kernels: 199 us -> 182 us  [per_device(): pl.pallas_call(functools.partial(body, n_dp, n_t, chunks), out_shape=(jax...]
where the time goes in v2:
time: 188 us
  Pallas kernels  182 us (97%)
  local copies, waits for them, and re-layouts  5.84 us (3%)
    pallas_call x1, Pallas kernels, per_device(): pl.pallas_call(functools.partial(body, n_dp, n_t, chunks), out_shape=(jax...  182 us
    unnamed x3, local copies, waits for them, and re-layouts  5.84 us

profile of v2, /device:TPU:0, one launch (start us, length us, event | category | flops | bytes accessed | tf_op | source)
XLA Modules:
  0.0 188.0 jit_solution(14897184908884728955)
XLA Ops:
  0.6 181.5 %shard_map.103 = (bf16[32,4096]{1,0:T(8,128)(2,1)}, f32[1,4096]{1,0:T(1,128)}, bf16[1792,512]{1,0:T(8,128)(2,1)}) custom-call(bf16[32,4096]{1,0:T(8,128)(2,1)} %tok_ref.1, bf16[32,4096]{1,0:T(8,128)(2,1)} %out_ref.1, bf16[128,1792]{1,0:T(8,128)(2,1)} %gate_ref.1, bf16[128,1792]{1,0:T(8,128)(2,1)} %up_ref.1, bf16[512,1792]{1,0:T(8,128)(2,1)} %wg_ref.1, ...), custom_call_target="tpu_custom_call" | custom-call | tf_op jit(solution)/shard_map/pallas_call | solution.py:559
  182.2 1.7 copy.14
  183.8 1.3 copy.15
  185.2 2.8 %copy.16 = bf16[1792,512]{1,0:T(8,128)(2,1)} copy(bf16[1792,512]{1,0:T(8,128)(2,1)} %get-tuple-element.14) | data formatting | bytes 3670016

commit v3 on v2

--- a/solution.py
+++ b/solution.py
@@ -43,6 +43,8 @@
     own,
     zsend,
     zin,
+    gp,
+    ga,
     gg,
     wrecv,
     npb,
@@ -61,6 +63,8 @@
     a_r,
     z_s,
     z_r,
+    p_s,
+    p_r,
     b_s,
     b_r,
     w_s,
@@ -155,9 +159,6 @@
     x4[d, t] = out_ref[:, col(d)]
     loop(n_t, lambda j: second_own(j).start(), 1)
 
-    gate = gate_ref[...].astype(F32)
-    aall[d] = (gate * jax.nn.sigmoid(gate) * up_ref[...].astype(F32)).astype(BF16)
-
     w_rows = cols // W_CHUNKS
 
     def weight_copy(n):
@@ -226,6 +227,7 @@
         loop(line, one)
 
     half = rows // 2
+    strip = 16
 
     def act_unit(src, side, c):
         return aall.at[src * 2 + side, pl.ds(c * half, half)]
@@ -234,12 +236,46 @@
         u = act_unit(src, y, c)
         return rcopy(u, u, a_s.at[2, src, c], a_r.at[2, src, c], pair, t)
 
+    def pre_unit(src, side, a):
+        return gp.at[src, a]
+
+    def pre_own(a, way):
+        return rcopy(
+            (gate_ref, up_ref)[a],
+            gp.at[z, a],
+            p_s.at[way, z, a],
+            p_r.at[way, z, a],
+            d + 2 - 4 * way,
+            t,
+        )
+
+    for a in range(2):
+
+        @pl.when(z < line - 1)
+        def _():
+            pre_own(a, 0).start()
+
+        @pl.when(z > 0)
+        def _():
+            pre_own(a, 1).start()
+
+    gp[z, 0] = gate_ref[...]
+    gp[z, 1] = up_ref[...]
+
+    def make_act(src):
+        def piece(n):
+            sl = pl.ds(n * strip, strip)
+            gate = gp[src, 0, sl].astype(F32)
+            aall[src * 2 + y, sl] = (
+                gate * jax.nn.sigmoid(gate) * gp[src, 1, sl].astype(F32)
+            ).astype(BF16)
+
+        loop(rows // strip, piece)
+        act_pair(src, 0).start()
+
+    make_act(z)
     act_pair(z, 1).start()
-    gather_own(act_unit, a_s, a_r, 0, y, 0)
-    gather_own(act_unit, a_s, a_r, 0, y, 1)
-    act_pair(z, 0).start()
-    for n in range(2):
-        weight_copy(n).start()
+    weight_copy(0).start()
 
     def relay(k):
         src = lax.rem(d + n_dp - k, n_dp)
@@ -284,17 +320,15 @@
 
     loop(line, keep)
 
-    weight_copy(2).start()
+    weight_copy(1).start()
 
     def act_step(s):
-        gather_step(
-            act_unit, a_s, a_r, 0, y, s, 0, lambda src: act_pair(src, 0).start()
-        )
-        gather_step(act_unit, a_s, a_r, 0, y, s, 1)
+        gather_step(pre_unit, p_s, p_r, 0, y, s, 0)
+        gather_step(pre_unit, p_s, p_r, 0, y, s, 1, make_act)
         gather_step(act_unit, a_s, a_r, 3, other, s, 1)
 
-    loop(line, act_step, 1)
-    for n in range(3, 2 * W_CHUNKS):
+    loop(line - 1, act_step, 1)
+    for n in range(2, 4):
         weight_copy(n).start()
 
     def line_part(way, zz, c):
@@ -341,7 +375,7 @@
     loop(line // 2, reduce_pairs)
 
     def grad_unit(src, side, c):
-        return gg.at[src, :, cs(c)]
+        return ga.at[src, cs(c)]
 
     for c in range(chunks):
 
@@ -355,14 +389,95 @@
             line_in(1, z, c)
             own[z, cs(c)] += zin[1, z, cs(c)].astype(F32)
 
-        grad_act = own[z, cs(c)]
-        gate = gate_ref[cs(c), :].astype(F32)
-        sig = jax.nn.sigmoid(gate)
-        gg[z, 0, cs(c)] = (
-            grad_act * up_ref[cs(c), :].astype(F32) * sig * (1.0 + gate * (1.0 - sig))
-        ).astype(BF16)
-        gg[z, 1, cs(c)] = (grad_act * (gate * sig)).astype(BF16)
+        ga[z, cs(c)] = own[z, cs(c)].astype(BF16)
         gather_own(grad_unit, b_s, b_r, 0, y, c)
+
+    act_step(line - 1)
+    for n in range(4, 2 * W_CHUNKS):
+        weight_copy(n).start()
+
+    def norm_copy(side, i, j):
+        tt = t_peer(j)
+        return rcopy(
+            npb.at[side, i, tt], nrv.at[side, i, t], n_s.at[side, i, j], n_r.at[side, i, t], d, tt
+        )
+
+    def norm_own(i):
+        def piece(n):
+            sl = pl.ds(n * strip, strip)
+            grad_act = ga[i, sl].astype(F32)
+            gate = gp[i, 0, sl].astype(F32)
+            sig = jax.nn.sigmoid(gate)
+            gg[i, 0, sl] = (
+                grad_act * gp[i, 1, sl].astype(F32) * sig * (1.0 + gate * (1.0 - sig))
+            ).astype(BF16)
+            gg[i, 1, sl] = (grad_act * (gate * sig)).astype(BF16)
+
+        loop(rows // strip, piece)
+        part = lax.dot_general(gg[i, 0], wg_ref[...], NT, preferred_element_type=F32)
+        part = part + lax.dot_general(gg[i, 1], wu_ref[...], NT, preferred_element_type=F32)
+        npb[y, i] = part.reshape(n_t, r, cols).astype(BF16)
+        loop(n_t, lambda j: norm_copy(y, i, j).start(), 1)
+
+    def norm_other(p):
+        two = pl.ds(2 * p, 2)
+        part = lax.dot_general(
+            gg[two, 0].reshape(2 * rows, hidden), wrecv[0], NT, preferred_element_type=F32
+        )
+        part = part + lax.dot_general(
+            gg[two, 1].reshape(2 * rows, hidden), wrecv[1], NT, preferred_element_type=F32
+        )
+        npb[other, two] = part.reshape(2, n_t, r, cols).astype(BF16)
+        loop(2, lambda q: loop(n_t, lambda j: norm_copy(other, 2 * p + q, j).start(), 1))
+
+    def fin_copy(side, i):
+        return rcopy(
+            gs.at[side, i], fin.at[z, side], f_s.at[side, i], f_r.at[side, z], i * 2 + y, t
+        )
+
+    def combine(side, i):
+        def add(j, acc):
+            tt = t_peer(j)
+            rcopy(
+                npb.at[side, i, tt], nrv.at[side, i, tt], n_s.at[side, i, 0], n_r.at[side, i, tt], d, t
+            ).wait_recv()
+            return acc + nrv[side, i, tt].astype(F32)
+
+        acc = lax.fori_loop(1, n_t, add, npb[side, i, t].astype(F32)).astype(BF16)
+
+        @pl.when(i != z)
+        def _():
+            gs[side, i] = acc
+            fin_copy(side, i).start()
+
+        @pl.when(i == z)
+        def _():
+            fin[z, side] = acc
+
+    def at_distance(dist, f):
+        def one(q):
+            src = jnp.where(q == 0, z - dist, z + dist)
+
+            @pl.when((src >= 0) & (src < line) & ((dist > 0) | (q == 0)))
+            def _():
+                f(src)
+
+        loop(2, one)
+
+    def visit(s):
+        @pl.when(s > 0)
+        def _():
+            for c in range(chunks):
+                gather_step(grad_unit, b_s, b_r, 0, y, s, c)
+
+        at_distance(s, norm_own)
+
+        @pl.when(s > 0)
+        def _():
+            at_distance(s - 1, lambda src: combine(y, src))
+
+    loop(line, visit)
+    at_distance(line - 1, lambda src: combine(y, src))
 
     loop(line, lambda src: arrived(act_unit, a_s, a_r, 2, src, other, 0))
     tile = 256 if hidden % 256 == 0 else hidden
@@ -382,80 +497,9 @@
 
     loop(hidden // tile, down_tile)
 
-    def norm_copy(side, i, j):
-        tt = t_peer(j)
-        return rcopy(
-            npb.at[side, i, tt], nrv.at[side, i, t], n_s.at[side, i, j], n_r.at[side, i, t], d, tt
-        )
-
-    def norm_own(i):
-        part = lax.dot_general(gg[i, 0], wg_ref[...], NT, preferred_element_type=F32)
-        part = part + lax.dot_general(gg[i, 1], wu_ref[...], NT, preferred_element_type=F32)
-        npb[y, i] = part.reshape(n_t, r, cols).astype(BF16)
-        loop(n_t, lambda j: norm_copy(y, i, j).start(), 1)
-
-    def norm_other(p):
-        two = pl.ds(2 * p, 2)
-        part = lax.dot_general(
-            gg[two, 0].reshape(2 * rows, hidden), wrecv[0], NT, preferred_element_type=F32
-        )
-        part = part + lax.dot_general(
-            gg[two, 1].reshape(2 * rows, hidden), wrecv[1], NT, preferred_element_type=F32
-        )
-        npb[other, two] = part.reshape(2, n_t, r, cols).astype(BF16)
-        loop(2, lambda q: loop(n_t, lambda j: norm_copy(other, 2 * p + q, j).start(), 1))
-
-    def fin_copy(side, i):
-        return rcopy(
-            gs.at[side, i], fin.at[z, side], f_s.at[side, i], f_r.at[side, z], i * 2 + y, t
-        )
-
-    def combine(side, i):
-        def add(j, acc):
-            tt = t_peer(j)
-            rcopy(
-                npb.at[side, i, tt], nrv.at[side, i, tt], n_s.at[side, i, 0], n_r.at[side, i, tt], d, t
-            ).wait_recv()
-            return acc + nrv[side, i, tt].astype(F32)
-
-        acc = lax.fori_loop(1, n_t, add, npb[side, i, t].astype(F32)).astype(BF16)
-
-        @pl.when(i != z)
-        def _():
-            gs[side, i] = acc
-            fin_copy(side, i).start()
-
-        @pl.when(i == z)
-        def _():
-            fin[z, side] = acc
-
-    def at_distance(dist, f):
-        def one(q):
-            src = jnp.where(q == 0, z - dist, z + dist)
-
-            @pl.when((src >= 0) & (src < line) & ((dist > 0) | (q == 0)))
-            def _():
-                f(src)
-
-        loop(2, one)
-
-    def visit(s):
-        @pl.when(s > 0)
-        def _():
-            for c in range(chunks):
-                gather_step(grad_unit, b_s, b_r, 0, y, s, c)
-
-        at_distance(s, norm_own)
-
-        @pl.when(s > 0)
-        def _():
-            at_distance(s - 1, lambda src: combine(y, src))
-
-    loop(line, visit)
     for n in range(2 * W_CHUNKS):
         weight_copy(n).wait_recv()
     loop(line // 2, norm_other)
-    at_distance(line - 1, lambda src: combine(y, src))
     loop(line, lambda i: combine(other, i))
 
     total = jnp.zeros((r, 1), F32)
@@ -518,7 +562,7 @@
     loop(n_dp, lambda k: first(k, dp_peer(k)).wait_send(), 1)
     loop(n_dp, lambda i: loop(n_t, lambda j: second(i, j).wait_send(), 1))
     for c in range(2):
-        gather_drain(act_unit, a_s, a_r, 0, y, c)
+        gather_drain(pre_unit, p_s, p_r, 0, y, c)
     gather_drain(act_unit, a_s, a_r, 3, other, 1)
     loop(line, lambda src: act_pair(src, 0).wait_send())
     act_pair(z, 1).wait_send()
@@ -544,6 +588,12 @@
     loop(2, drain_norm)
     loop(n_t, lambda j: gain_copy(j).wait_send(), 1)
     loop(n_dp, lambda k: all_copy(k).wait_send(), 1)
+
+
+def hand_on(ig_in, gain_in, dg_in, ig_out, gain_out, dg_out):
+    ig_out[...] = ig_in[...]
+    gain_out[...] = gain_in[...].reshape(gain_out.shape)
+    dg_out[...] = dg_in[...]
 
 
 def per_device(
@@ -575,6 +625,8 @@
             pltpu.VMEM((line, rows, hidden), BF16),
             pltpu.VMEM((2, line, rows, hidden), BF16),
             pltpu.VMEM((line, 2, rows, hidden), BF16),
+            pltpu.VMEM((line, rows, hidden), BF16),
+            pltpu.VMEM((line, 2, rows, hidden), BF16),
             pltpu.VMEM((2, cols, hidden), BF16),
             pltpu.VMEM((2, line, n_t, r, cols), BF16),
             pltpu.VMEM((2, line, n_t, r, cols), BF16),
@@ -592,6 +644,8 @@
             dma((5, line, 2)),
             dma((line, chunks)),
             dma((2, line, chunks)),
+            dma((2, line, 2)),
+            dma((2, line, 2)),
             dma((2, line, chunks)),
             dma((2, line, chunks)),
             dma((2, W_CHUNKS)),
@@ -618,7 +672,16 @@
         down_weight,
         norm_gain.reshape(1, width),
     )
-    return (input_grad, gain_grad.reshape(width), down_grad)
+    return pl.pallas_call(
+        hand_on,
+        out_shape=(
+            jax.ShapeDtypeStruct((r, width), BF16),
+            jax.ShapeDtypeStruct((width,), F32),
+            jax.ShapeDtypeStruct((hidden, cols), BF16),
+        ),
+        in_specs=[vmem] * 3,
+        out_specs=(vmem, vmem, vmem),
+    )(input_grad, gain_grad, down_grad)
 
 
 def solution(mesh):

time: 188 us -> 185 us (0.984)
  local copies, waits for them, and re-layouts: 5.84 us -> 0 us
  Pallas kernels: 182 us -> 184 us
    unnamed x3 -> x0, local copies, waits for them, and re-layouts: 5.84 us -> none
    pallas_call x0 -> x1, Pallas kernels: none -> 2.98 us  [per_device(): pl.pallas_call(hand_on, out_shape=(jax.ShapeDtypeStruct((r, width), BF16)...]
where the time goes in v3:
time: 185 us
  Pallas kernels  184 us (99%)
    pallas_call x1, Pallas kernels, per_device(): pl.pallas_call(functools.partial(body, n_dp, n_t, chunks), out_shape=(jax...  181 us

profile of v3, /device:TPU:0, one launch (start us, length us, event | category | flops | bytes accessed | tf_op | source)
XLA Modules:
  0.0 184.8 jit_solution(2745363322741330447)
XLA Ops:
  0.6 181.1 %shard_map.103 = (bf16[32,4096]{1,0:T(8,128)(2,1)}, f32[1,4096]{1,0:T(1,128)}, bf16[1792,512]{1,0:T(8,128)(2,1)}) custom-call(bf16[32,4096]{1,0:T(8,128)(2,1)} %tok_ref.1, bf16[32,4096]{1,0:T(8,128)(2,1)} %out_ref.1, bf16[128,1792]{1,0:T(8,128)(2,1)} %gate_ref.1, bf16[128,1792]{1,0:T(8,128)(2,1)} %up_ref.1, bf16[512,1792]{1,0:T(8,128)(2,1)} %wg_ref.1, ...), custom_call_target="tpu_custom_call" | custom-call | tf_op jit(solution)/shard_map/pallas_call | solution.py:609
  181.8 3.0 %shard_map.104 = (bf16[32,4096]{1,0:T(8,128)(2,1)}, f32[4096]{0:T(1024)}, bf16[1792,512]{1,0:T(8,128)(2,1)}) custom-call(bf16[32,4096]{1,0:T(8,128)(2,1)} %get-tuple-element.6.ig_in, f32[1,4096]{1,0:T(1,128)} %get-tuple-element.7.gain_in, bf16[1792,512]{1,0:T(8,128)(2,1)} %get-tuple-element.8.dg_in), custom_call_target="tpu_custom_call" | custom-call | tf_op jit(solution)/shard_map/pallas_call | solution.py:675

commit v4 on v3

--- a/solution.py
+++ b/solution.py
@@ -226,11 +226,12 @@
 
         loop(line, one)
 
-    half = rows // 2
+    far = rows * 3 // 4
     strip = 16
 
     def act_unit(src, side, c):
-        return aall.at[src * 2 + side, pl.ds(c * half, half)]
+        at = (0, rows - far)[c]
+        return aall.at[src * 2 + side, pl.ds(at, (rows - far, far)[c])]
 
     def act_pair(src, c):
         u = act_unit(src, y, c)

time: 185 us -> 177 us (0.957)
  Pallas kernels: 184 us -> 177 us
    pallas_call x1, Pallas kernels: 181 us -> 174 us  [per_device(): pl.pallas_call(functools.partial(body, n_dp, n_t, chunks), out_shape=(jax...]
where the time goes in v4:
time: 177 us
  Pallas kernels  177 us (100%)
    pallas_call x1, Pallas kernels, per_device(): pl.pallas_call(functools.partial(body, n_dp, n_t, chunks), out_shape=(jax...  174 us

profile of v4, /device:TPU:0, one launch (start us, length us, event | category | flops | bytes accessed | tf_op | source)
XLA Modules:
  0.0 177.2 jit_solution(16446836537873436509)
XLA Ops:
  0.6 173.6 %shard_map.103 = (bf16[32,4096]{1,0:T(8,128)(2,1)}, f32[1,4096]{1,0:T(1,128)}, bf16[1792,512]{1,0:T(8,128)(2,1)}) custom-call(bf16[32,4096]{1,0:T(8,128)(2,1)} %tok_ref.1, bf16[32,4096]{1,0:T(8,128)(2,1)} %out_ref.1, bf16[128,1792]{1,0:T(8,128)(2,1)} %gate_ref.1, bf16[128,1792]{1,0:T(8,128)(2,1)} %up_ref.1, bf16[512,1792]{1,0:T(8,128)(2,1)} %wg_ref.1, ...), custom_call_target="tpu_custom_call" | custom-call | tf_op jit(solution)/shard_map/pallas_call | solution.py:610
  174.2 3.0 %shard_map.104 = (bf16[32,4096]{1,0:T(8,128)(2,1)}, f32[4096]{0:T(1024)}, bf16[1792,512]{1,0:T(8,128)(2,1)}) custom-call(bf16[32,4096]{1,0:T(8,128)(2,1)} %get-tuple-element.6.ig_in, f32[1,4096]{1,0:T(1,128)} %get-tuple-element.7.gain_in, bf16[1792,512]{1,0:T(8,128)(2,1)} %get-tuple-element.8.dg_in), custom_call_target="tpu_custom_call" | custom-call | tf_op jit(solution)/shard_map/pallas_call | solution.py:676
